TPU v7x, 32 devices: a whole 2x2x4 slice. The times are simulated.
32 devices in a mesh: dap: 8 (over z, x), cplx: 4 (over y, core).
Axes of the slice: x: 2, y: 2, z: 4, core: 2. Of those that a mesh axis runs over, the one named last changes fastest.
Arguments:
- pair: bfloat16 [96, 384, 128], P('dap', 'cplx'), parts along dimension 1, may hold values from -6 to 6
- cotangent: bfloat16 [96, 384, 128], P('dap', 'cplx'), parts along dimension 1, may hold values from -6 to 6
- residue_mask: int32 [384], P('cplx'), parts along dimension 0, may hold values 0 or 1
- chain_ids: int32 [384], P('cplx'), parts along dimension 0, may hold values from 0 to 2, never falling along the last dimension, each value on 1 to 48 neighbouring positions
- chain_embed: float32 [2, 128], replicated, may hold values from -4 to 4
- out_norm_gain: float32 [128], replicated, may hold values from 0.25 to 1.75
- out_proj: bfloat16 [128, 512], replicated, may hold values from -0.5 to 0.5
- out_gate: bfloat16 [128, 128], replicated, may hold values from -0.5 to 0.5
- out_mid_gain: float32 [128], replicated, may hold values from 0.25 to 1.75
- out_final: bfloat16 [128, 128], replicated, may hold values from -0.5 to 0.5
- in_norm_gain: float32 [128], replicated, may hold values from 0.25 to 1.75
- in_proj: bfloat16 [128, 512], replicated, may hold values from -0.5 to 0.5
- in_gate: bfloat16 [128, 128], replicated, may hold values from -0.5 to 0.5
- in_mid_gain: float32 [128], replicated, may hold values from 0.25 to 1.75
- in_final: bfloat16 [128, 128], replicated, may hold values from -0.5 to 0.5
Outputs:
- pair_grad: bfloat16 [96, 384, 128], P('dap', 'cplx'), parts along dimension 1
- grad_proj: float32 [512, 512], P('cplx'), parts along dimension 0
- grad_gate: float32 [512, 128], P('cplx'), parts along dimension 0
- grad_final: float32 [512, 128], P('cplx'), parts along dimension 0
- grad_norm_gain: float32 [512], P('cplx'), parts along dimension 0
- grad_mid_gain: float32 [512], P('cplx'), parts along dimension 0
There are 4 independent parts, one for each index of `cplx`. A program takes and returns all parts, laid end to end along the dimension named above; an argument that names none is the same for every part. Nothing has to cross between parts.
Inputs may be any that keep to these rules, and one draw needn't show every extreme that they name: `chain_ids`: chain numbers never fall along the residues; each chain has at most 48 residues.
All inputs are finite; a program needn't handle non-finite values.
Results may differ from a plain program's by a relative error of at most 0.019.
Values may be sent and summed in bfloat16 or wider, within the bound.
A program may use at most 128 MiB of HBM per device.

v0:
```python
import jax
import jax.numpy as jnp
from jax import lax
from jax.sharding import PartitionSpec as P


def layer_norm(values_in, gain):
    average = jnp.mean(values_in, axis=-1, keepdims=True)
    centred = values_in - average
    variance = jnp.mean(centred * centred, axis=-1, keepdims=True)
    return centred * lax.rsqrt(variance + 1e-05) * gain


def gated_pair(projected, pair_mask, hidden_width):
    masked = pair_mask[..., None]
    left_act = (
        masked
        * jax.nn.sigmoid(projected[..., :hidden_width])
        * projected[..., hidden_width : 2 * hidden_width]
    )
    right_act = (
        masked
        * jax.nn.sigmoid(projected[..., 2 * hidden_width : 3 * hidden_width])
        * projected[..., 3 * hidden_width :]
    )
    return (left_act, right_act)


def shards(
    pair,
    cotangent,
    residue_mask,
    chain_ids,
    chain_embed,
    out_norm_gain,
    out_proj,
    out_gate,
    out_mid_gain,
    out_final,
    in_norm_gain,
    in_proj,
    in_gate,
    in_mid_gain,
    in_final,
):
    f32 = jnp.float32
    bf16 = jnp.bfloat16
    row_count = pair.shape[0]
    res_count = pair.shape[1]
    hidden_width = out_final.shape[0]
    inv_count = 1.0 / res_count
    row_start = lax.axis_index("dap") * row_count
    row_mask = lax.dynamic_slice_in_dim(residue_mask, row_start, row_count, 0)
    row_chain = lax.dynamic_slice_in_dim(chain_ids, row_start, row_count, 0)
    pair_mask = (row_mask[:, None] * residue_mask[None, :]).astype(f32)
    same_chain = row_chain[:, None] == chain_ids[None, :]
    start = pair.astype(f32) + jnp.where(same_chain[..., None], chain_embed[1], chain_embed[0])
    out_normed = layer_norm(start, out_norm_gain).astype(bf16)
    projected = jnp.dot(out_normed, out_proj, preferred_element_type=f32)
    left_act, right_act = gated_pair(projected, pair_mask, hidden_width)
    left_b = left_act.astype(bf16)
    right_b = right_act.astype(bf16)
    x_out = jnp.einsum(
        "ikc,jkc->ijc",
        left_b,
        lax.all_gather(right_b, "dap", axis=0, tiled=True),
        preferred_element_type=f32,
    )
    y_out = layer_norm(x_out, out_mid_gain).astype(bf16)
    update = jax.nn.sigmoid(jnp.dot(out_normed, out_gate, preferred_element_type=f32)) * jnp.dot(
        y_out, out_final, preferred_element_type=f32
    )
    pair_mid = (start + update).astype(bf16)
    mid_f32 = pair_mid.astype(f32)
    normed_f32, norm_back = jax.vjp(layer_norm, mid_f32, in_norm_gain)
    in_normed = normed_f32.astype(bf16)
    proj_in = jnp.dot(in_normed, in_proj, preferred_element_type=f32)
    (left_in, right_in), glu_back = jax.vjp(
        lambda proj_val: gated_pair(proj_val, pair_mask, hidden_width), proj_in
    )
    left_ib = left_in.astype(bf16)
    right_ib = right_in.astype(bf16)
    columns = lax.all_to_all(left_ib, "dap", split_axis=1, concat_axis=0, tiled=True)
    left_block = columns
    x_in = jnp.einsum(
        "kic,kjc->ijc",
        left_block,
        lax.all_gather(right_ib, "dap", axis=0, tiled=True),
        preferred_element_type=f32,
    )
    y_f32, mid_back = jax.vjp(layer_norm, x_in, in_mid_gain)
    y_in = y_f32.astype(bf16)
    logit = jnp.dot(in_normed, in_gate, preferred_element_type=f32)
    value = jnp.dot(y_in, in_final, preferred_element_type=f32)
    sigma = jax.nn.sigmoid(logit)
    upstream = cotangent.astype(f32)
    grad_value = (upstream * sigma).astype(bf16)
    grad_logit = (upstream * value * sigma * (1.0 - sigma)).astype(bf16)
    grad_final = jnp.einsum("ijc,ijd->cd", y_in, grad_value, preferred_element_type=f32) * inv_count
    grad_gate = (
        jnp.einsum("ijc,ijd->cd", in_normed, grad_logit, preferred_element_type=f32) * inv_count
    )
    grad_y = jnp.dot(grad_value, in_final.T, preferred_element_type=f32)
    grad_x, grad_mid = mid_back(grad_y)
    grad_x_b = grad_x.astype(bf16)
    shard_rows = lax.all_gather(grad_x_b, "dap", axis=0, tiled=True)
    left_block = left_ib
    grad_right = jnp.einsum("kic,ijc->kjc", left_block, shard_rows, preferred_element_type=f32)
    new_block = jnp.einsum("kjc,ijc->kic", right_ib, shard_rows, preferred_element_type=f32)
    grad_p = glu_back((new_block, grad_right))[0].astype(bf16)
    grad_proj = jnp.einsum("ijc,ijd->cd", in_normed, grad_p, preferred_element_type=f32) * inv_count
    grad_normed = jnp.dot(grad_p, in_proj.T, preferred_element_type=f32) + jnp.dot(
        grad_logit, in_gate.T, preferred_element_type=f32
    )
    grad_z, grad_norm = norm_back(grad_normed)
    pair_grad = (upstream + grad_z).astype(bf16)
    reduced = (
        lax.psum(grad_proj.astype(jnp.bfloat16), "dap").astype(jnp.float32),
        lax.psum(grad_gate.astype(jnp.bfloat16), "dap").astype(jnp.float32),
        lax.psum(grad_final.astype(jnp.bfloat16), "dap").astype(jnp.float32),
        lax.psum((grad_norm * inv_count).astype(jnp.bfloat16), "dap").astype(jnp.float32),
        lax.psum((grad_mid * inv_count).astype(jnp.bfloat16), "dap").astype(jnp.float32),
    )
    return (pair_grad, reduced[0], reduced[1], reduced[2], reduced[3], reduced[4])


def solution(mesh):
    placed = (
        P("dap", "cplx", None),
        P("dap", "cplx", None),
        P("cplx"),
        P("cplx"),
        P(),
        P(),
        P(),
        P(),
        P(),
        P(),
        P(),
        P(),
        P(),
        P(),
        P(),
    )
    return jax.shard_map(
        shards,
        mesh=mesh,
        in_specs=placed,
        out_specs=(
            P("dap", "cplx", None),
            P("cplx", None),
            P("cplx", None),
            P("cplx", None),
            P("cplx"),
            P("cplx"),
        ),
        check_vma=False,
    )
```

profile of v0, /device:TPU:0, one launch (start us, length us, event | category | flops | bytes accessed | tf_op | source)
XLA Modules:
  0.0 371.3 jit_solution(1143531026395006253)
XLA Ops:
  10.9 1.6 multiply_reduce_fusion.7
  13.9 1.9 fusion.47
  18.3 1.7 fusion.8
  19.9 51.8 %all-gather.4.cloned.1.call-done = bf16[96,96,128]{2,1,0:T(8,128)(2,1)} async-done(((bf16[12,96,128]{2,1,0:T(8,128)(2,1)}), bf16[96,96,128]{2,1,0:T(8,128)(2,1)}) %all-gather.4.cloned.1.call-update) | async-done | bytes 2359312 | tf_op jit(solution)/shard_map/all_gather | solution.py:66
  71.7 3.5 copy.46
  75.2 2.8 fusion.62
  84.9 3.5 all-to-all-start
  89.5 17.3 %all-to-all-done = bf16[12,96,128]{2,0,1:T(8,128)(2,1)S(1)} async-done(((bf16[12,96,128]{2,0,1:T(8,128)(2,1)}), bf16[12,96,128]{2,0,1:T(8,128)(2,1)S(1)}, u32[]{:S(2)}, u32[]{:S(2)}) %all-to-all-start) | async-done | bytes 294944 | tf_op jit(solution)/shard_map/all_to_all | solution.py:83
  108.2 29.5 %all-gather.6.cloned.1.call-done = bf16[96,96,128]{2,1,0:T(8,128)(2,1)} async-done(((bf16[12,96,128]{2,1,0:T(8,128)(2,1)}), bf16[96,96,128]{2,1,0:T(8,128)(2,1)}) %all-gather.6.cloned.1.call-update) | async-done | bytes 2359312 | tf_op jit(solution)/shard_map/all_gather | solution.py:88
  137.7 3.5 copy.52
  141.3 3.0 fusion.64
  144.2 1.6 copy.54
  147.7 1.5 add_convert_fusion.1
  155.7 44.1 %all-gather.8.cloned.1.call-done = bf16[96,96,128]{2,1,0:T(8,128)(2,1)} async-done(((bf16[12,96,128]{2,1,0:T(8,128)(2,1)}), bf16[96,96,128]{2,1,0:T(8,128)(2,1)}) %all-gather.8.cloned.1.call-update) | async-done | bytes 2359312 | tf_op jit(solution)/shard_map/all_gather | solution.py:106
  199.8 3.5 copy.55
  203.3 3.8 %fusion.66 = f32[128,96,12]{1,2,0:T(8,128)} fusion(bf16[96,96,128]{1,0,2:T(8,128)(2,1)S(1)} %copy.55, bf16[12,96,128]{1,0,2:T(8,128)(2,1)} %copy.59), kind=kOutput, calls=%fused_computation.126 | convolution fusion | flops 28311552 | bytes 3244032 | tf_op jit(solution)/shard_map/kjc,ijc->kic/dot_general | solution.py:109
  207.1 2.4 copy.60
  209.4 2.9 fusion.65
  212.4 1.5 copy.57
  213.9 2.4 bitcast_multiply_fusion.3
  220.8 1.5 fusion.19
  222.3 66.6 %all-reduce.10.cloned.1.call-done = (bf16[128,128]{1,0:T(8,128)(2,1)}, bf16[128,128]{1,0:T(8,128)(2,1)}, bf16[128]{0:T(256)(128)(2,1)}, bf16[128]{0:T(256)(128)(2,1)}) async-done(((bf16[128,128]{1,0:T(8,128)(2,1)}, bf16[128,128]{1,0:T(8,128)(2,1)}, bf16[128]{0:T(256)(128)(2,1)}, bf16[128]{0:T(256)(128)(2,1)}), (bf16[128,128]{1,0:T(8,128)(2,1)}, bf16[128,128]{1,0:T(8,128)(2,1)}, bf16[128]{0:T(256)(128)(2,1)}, ...) | async-done | bytes 66064 | tf_op jit(solution)/shard_map/psum | solution.py:119
  293.9 69.3 %all-reduce.8.cloned.1.call-done = bf16[128,512]{1,0:T(8,128)(2,1)} async-done(((bf16[128,512]{1,0:T(8,128)(2,1)}), bf16[128,512]{1,0:T(8,128)(2,1)}) %all-reduce.8.cloned.1.call-update) | async-done | bytes 131088 | tf_op jit(solution)/shard_map/psum | solution.py:118
  363.2 1.6 convert_element_type.107
  (111 shorter events, 34.5 us)
Async XLA Ops:
  7.2 73.9 %copy-start = (bf16[128,512]{1,0:T(8,128)(2,1)S(1)}, bf16[128,512]{1,0:T(8,128)(2,1)}, u32[]{:S(2)}) copy-start(bf16[128,512]{1,0:T(8,128)(2,1)} %param.26) | copy-start | bytes 393220
  7.2 64.5 %all-gather.4.cloned.1.call-start = ((), (), s32[]{:S(2)}) async-start(), calls=%async_computation.1 | async-start | bytes 2654208 | tf_op jit(solution)/shard_map/all_gather | solution.py:66
  15.9 2.4 copy-start.5
  15.9 2.4 copy-start.23
  15.9 2.4 copy-start.25
  17.0 120.7 %all-gather.6.cloned.1.call-start = ((), (), s32[]{:S(2)}) async-start(), calls=%async_computation.2 | async-start | bytes 2654208 | tf_op jit(solution)/shard_map/all_gather | solution.py:88
  75.2 3.1 copy-start.24
  78.1 2.6 copy-start.22
  81.1 7.4 %copy-start.14 = (bf16[12,96,128]{2,1,0:T(8,128)(2,1)}, bf16[12,96,128]{2,1,0:T(8,128)(2,1)S(1)}, u32[]{:S(2)}) copy-start(bf16[12,96,128]{2,1,0:T(8,128)(2,1)S(1)} %multiply_convert_fusion.4) | copy-start | bytes 884740
  81.5 1.4 copy-start.1
  82.9 5.5 %copy-start.20 = (bf16[128,128]{1,0:T(8,128)(2,1)S(1)}, bf16[128,128]{1,0:T(8,128)(2,1)}, u32[]{:S(2)}) copy-start(bf16[128,128]{1,0:T(8,128)(2,1)} %param.27) | copy-start | bytes 98308
  84.0 22.9 %copy-start.9 = (bf16[12,96,128]{2,1,0:T(8,128)(2,1)}, bf16[12,96,128]{2,1,0:T(8,128)(2,1)S(1)}, u32[]{:S(2)}) copy-start(bf16[12,96,128]{2,1,0:T(8,128)(2,1)S(1)} %get-tuple-element.22) | copy-start | bytes 884740
  84.9 22.0 %all-to-all-start = ((bf16[12,96,128]{2,0,1:T(8,128)(2,1)}), bf16[12,96,128]{2,0,1:T(8,128)(2,1)S(1)}, u32[]{:S(2)}, u32[]{:S(2)}) async-start(bf16[12,96,128]{2,0,1:T(8,128)(2,1)} %copy.49), calls=%async_computation | async-start | bytes 786432 | tf_op jit(solution)/shard_map/all_to_all | solution.py:83
  88.4 111.4 %all-gather.8.cloned.1.call-start = ((), (), s32[]{:S(2)}) async-start(), calls=%async_computation.3 | async-start | bytes 2654208 | tf_op jit(solution)/shard_map/all_gather | solution.py:106
  141.2 4.9 %copy-start.18 = (bf16[128,128]{1,0:T(8,128)(2,1)S(1)}, bf16[128,128]{1,0:T(8,128)(2,1)}, u32[]{:S(2)}) copy-start(bf16[128,128]{1,0:T(8,128)(2,1)} %param.29) | copy-start | bytes 98308
  141.2 4.9 %copy-start.21 = (f32[128]{0:T(128)S(1)}, f32[128]{0:T(128)}, u32[]{:S(2)}) copy-start(f32[128]{0:T(128)} %param.28) | copy-start | bytes 1540
  144.2 1.9 copy-start.4
  144.2 1.9 copy-start.7
  146.2 3.2 copy-start.11
  146.9 3.7 %copy-start.10 = (bf16[12,96,128]{2,1,0:T(8,128)(2,1)S(1)}, bf16[12,96,128]{2,1,0:T(8,128)(2,1)}, u32[]{:S(2)}) copy-start(bf16[12,96,128]{2,1,0:T(8,128)(2,1)} %copy-done.9) | copy-start | bytes 884740
  147.7 5.9 %copy-start.15 = (bf16[12,96,128]{2,1,0:T(8,128)(2,1)S(1)}, bf16[12,96,128]{2,1,0:T(8,128)(2,1)}, u32[]{:S(2)}) copy-start(bf16[12,96,128]{2,1,0:T(8,128)(2,1)} %copy-done.14) | copy-start | bytes 884740
  149.2 139.7 %all-reduce.10.cloned.1.call-start = ((), (), s32[]{:S(2)}) async-start(), calls=%async_computation.5 | async-start | bytes 133120 | tf_op jit(solution)/shard_map/psum | solution.py:119
  218.3 2.5 copy-start.8
  220.2 143.0 %all-reduce.8.cloned.1.call-start = ((), (), s32[]{:S(2)}) async-start(), calls=%async_computation.4 | async-start | bytes 262144 | tf_op jit(solution)/shard_map/psum | solution.py:118
  (8 other events, 8.0 us)
Sparse Core Ops, SparseCore 0:
  17.1 54.5 all-gather.3
  84.1 53.5 all-gather.5
  149.3 50.4 all-gather.7
  220.3 68.4 all-reduce.9
  292.6 70.4 all-reduce.7
where the time goes:
time: 372 us; the launch traced here: 371 us
  waiting for transfers between devices  279 us (75%)
  local copies, waits for them, and re-layouts  27.9 us (8%)
  matrix products  23.6 us (6%)
  other arithmetic  22.7 us (6%)
  between operations  14.2 us (4%)
  starting transfers between devices  3.84 us (1%)
    psum x1, waiting for transfers between devices, shards(): lax.psum(grad_proj.astype(jnp.bfloat16), 'dap').astype(jnp.float32)  69.3 us
    psum x1, waiting for transfers between devices, shards(): lax.psum(grad_gate.astype(jnp.bfloat16), 'dap').astype(jnp.float32)  66.6 us
    all_gather x1, waiting for transfers between devices, shards(): lax.all_gather(right_b, 'dap', axis=0, tiled=True)  51.8 us
    all_gather x1, waiting for transfers between devices, shards(): shard_rows = lax.all_gather(grad_x_b, 'dap', axis=0, tiled=True)  44.1 us
    all_gather x1, waiting for transfers between devices, shards(): lax.all_gather(right_ib, 'dap', axis=0, tiled=True)  29.5 us
    all_to_all x1, waiting for transfers between devices, shards(): lax.all_to_all(left_ib, 'dap', split_axis=1, concat_axis=0, tiled=True)  17.3 us
  transfers between devices with their start and end apart: 6, of which 6 were waited for; matrix products, arithmetic and copies ran while one was open for 5% of the time, Pallas kernels for 0%

commit v1 on v0

--- a/solution.py
+++ b/solution.py
@@ -115,7 +115,7 @@
     grad_z, grad_norm = norm_back(grad_normed)
     pair_grad = (upstream + grad_z).astype(bf16)
     reduced = (
-        lax.psum(grad_proj.astype(jnp.bfloat16), "dap").astype(jnp.float32),
+        jnp.sum(lax.all_gather(grad_proj.astype(jnp.bfloat16), "dap"), axis=0).astype(jnp.float32),
         lax.psum(grad_gate.astype(jnp.bfloat16), "dap").astype(jnp.float32),
         lax.psum(grad_final.astype(jnp.bfloat16), "dap").astype(jnp.float32),
         lax.psum((grad_norm * inv_count).astype(jnp.bfloat16), "dap").astype(jnp.float32),

time: 372 us -> 341 us (0.917)
  waiting for transfers between devices: 279 us -> 245 us
    psum x1 -> x0, waiting for transfers between devices: 69.3 us -> none  [shards(): lax.psum(grad_proj.astype(jnp.bfloat16), 'dap').astype(jnp.float32)]
    all_gather x0 -> x1, waiting for transfers between devices: none -> 37.8 us  [shards(): lax.all_gather(grad_proj.astype(jnp.bfloat16), 'dap')]
  transfers between devices with their start and end apart: 6 -> 6, of which waited for: 6 -> 6; matrix products, arithmetic and copies ran while one was open for 5% -> 6% of each run, Pallas kernels for 0% -> 0%
where the time goes in v1:
time: 341 us; the launch traced here: 340 us
  waiting for transfers between devices  245 us (72%)
  local copies, waits for them, and re-layouts  28.4 us (8%)
  matrix products  24.8 us (7%)
  other arithmetic  23.2 us (7%)
  between operations  14.3 us (4%)
  starting transfers between devices  3.84 us (1%)
    psum x1, waiting for transfers between devices, shards(): lax.psum(grad_gate.astype(jnp.bfloat16), 'dap').astype(jnp.float32)  64.8 us
    all_gather x1, waiting for transfers between devices, shards(): lax.all_gather(right_b, 'dap', axis=0, tiled=True)  51.8 us
    all_gather x1, waiting for transfers between devices, shards(): shard_rows = lax.all_gather(grad_x_b, 'dap', axis=0, tiled=True)  44.1 us
    all_gather x1, waiting for transfers between devices, shards(): lax.all_gather(grad_proj.astype(jnp.bfloat16), 'dap')  37.8 us
    all_gather x1, waiting for transfers between devices, shards(): lax.all_gather(right_ib, 'dap', axis=0, tiled=True)  29.5 us
    all_to_all x1, waiting for transfers between devices, shards(): lax.all_to_all(left_ib, 'dap', split_axis=1, concat_axis=0, tiled=True)  17.3 us
  transfers between devices with their start and end apart: 6, of which 6 were waited for; matrix products, arithmetic and copies ran while one was open for 6% of the time, Pallas kernels for 0%

profile of v1, /device:TPU:0, one launch (start us, length us, event | category | flops | bytes accessed | tf_op | source)
XLA Modules:
  0.0 339.9 jit_solution(6143862542057024639)
XLA Ops:
  10.9 1.6 multiply_reduce_fusion.7
  13.9 1.9 fusion.47
  18.2 1.7 fusion.8
  19.9 51.8 %all-gather.6.cloned.1.call-done = bf16[96,96,128]{2,1,0:T(8,128)(2,1)} async-done(((bf16[12,96,128]{2,1,0:T(8,128)(2,1)}), bf16[96,96,128]{2,1,0:T(8,128)(2,1)}) %all-gather.6.cloned.1.call-update) | async-done | bytes 2359312 | tf_op jit(solution)/shard_map/all_gather | solution.py:66
  71.7 3.5 %copy.46 = bf16[96,96,128]{1,0,2:T(8,128)(2,1)S(1)} copy(bf16[96,96,128]{2,1,0:T(8,128)(2,1)} %all-gather.6.cloned.1.call-done) | data formatting | bytes 4718592 | tf_op jit(solution)/shard_map/all_gather | solution.py:66
  75.2 2.8 fusion.62
  84.9 3.5 %all-to-all-start = ((bf16[12,96,128]{2,0,1:T(8,128)(2,1)}), bf16[12,96,128]{2,0,1:T(8,128)(2,1)S(1)}, u32[]{:S(2)}, u32[]{:S(2)}) async-start(bf16[12,96,128]{2,0,1:T(8,128)(2,1)} %copy.49), calls=%async_computation | async-start | bytes 786432 | tf_op jit(solution)/shard_map/all_to_all | solution.py:83
  89.6 17.3 %all-to-all-done = bf16[12,96,128]{2,0,1:T(8,128)(2,1)S(1)} async-done(((bf16[12,96,128]{2,0,1:T(8,128)(2,1)}), bf16[12,96,128]{2,0,1:T(8,128)(2,1)S(1)}, u32[]{:S(2)}, u32[]{:S(2)}) %all-to-all-start) | async-done | bytes 294944 | tf_op jit(solution)/shard_map/all_to_all | solution.py:83
  108.3 29.5 %all-gather.8.cloned.1.call-done = bf16[96,96,128]{2,1,0:T(8,128)(2,1)} async-done(((bf16[12,96,128]{2,1,0:T(8,128)(2,1)}), bf16[96,96,128]{2,1,0:T(8,128)(2,1)}) %all-gather.8.cloned.1.call-update) | async-done | bytes 2359312 | tf_op jit(solution)/shard_map/all_gather | solution.py:88
  137.7 3.5 %copy.52 = bf16[96,96,128]{1,0,2:T(8,128)(2,1)S(1)} copy(bf16[96,96,128]{2,1,0:T(8,128)(2,1)} %all-gather.8.cloned.1.call-done) | data formatting | bytes 4718592 | tf_op jit(solution)/shard_map/all_gather | solution.py:88
  141.3 2.9 fusion.64
  144.2 1.6 copy.54
  147.7 1.4 add_convert_fusion.1
  155.7 44.1 %all-gather.10.cloned.1.call-done = bf16[96,96,128]{2,1,0:T(8,128)(2,1)} async-done(((bf16[12,96,128]{2,1,0:T(8,128)(2,1)}), bf16[96,96,128]{2,1,0:T(8,128)(2,1)}) %all-gather.10.cloned.1.call-update) | async-done | bytes 2359312 | tf_op jit(solution)/shard_map/all_gather | solution.py:106
  199.8 3.5 %copy.55 = bf16[96,96,128]{1,0,2:T(8,128)(2,1)S(1)} copy(bf16[96,96,128]{2,1,0:T(8,128)(2,1)} %all-gather.10.cloned.1.call-done) | data formatting | bytes 4718592 | tf_op jit(solution)/shard_map/all_gather | solution.py:106
  203.3 3.8 %fusion.66 = f32[128,96,12]{1,2,0:T(8,128)} fusion(bf16[96,96,128]{1,0,2:T(8,128)(2,1)S(1)} %copy.55, bf16[12,96,128]{1,0,2:T(8,128)(2,1)} %copy.59), kind=kOutput, calls=%fused_computation.126 | convolution fusion | flops 28311552 | bytes 3244032 | tf_op jit(solution)/shard_map/kjc,ijc->kic/dot_general | solution.py:109
  207.1 2.4 copy.60
  209.5 2.9 fusion.65
  212.4 1.5 copy.57
  213.9 2.4 bitcast_multiply_fusion.3
  219.8 2.3 fusion.13
  222.2 1.5 fusion.19
  223.6 64.8 %all-reduce.7.cloned.1.call-done = (bf16[128,128]{1,0:T(8,128)(2,1)}, bf16[128,128]{1,0:T(8,128)(2,1)}, bf16[128]{0:T(256)(128)(2,1)}, bf16[128]{0:T(256)(128)(2,1)}) async-done(((bf16[128,128]{1,0:T(8,128)(2,1)}, bf16[128,128]{1,0:T(8,128)(2,1)}, bf16[128]{0:T(256)(128)(2,1)}, bf16[128]{0:T(256)(128)(2,1)}), (bf16[128,128]{1,0:T(8,128)(2,1)}, bf16[128,128]{1,0:T(8,128)(2,1)}, bf16[128]{0:T(256)(128)(2,1)}, ...) | async-done | bytes 66064 | tf_op jit(solution)/shard_map/psum | solution.py:119
  293.5 37.8 %all-gather.12.cloned.1.call-done = bf16[1024,512]{1,0:T(8,128)(2,1)} async-done(((bf16[128,512]{1,0:T(8,128)(2,1)}), bf16[1024,512]{1,0:T(8,128)(2,1)}) %all-gather.12.cloned.1.call-update) | async-done | bytes 1048592 | tf_op jit(solution)/shard_map/all_gather | solution.py:118
  (116 shorter events, 35.7 us)
Async XLA Ops:
  7.2 73.9 %copy-start = (bf16[128,512]{1,0:T(8,128)(2,1)S(1)}, bf16[128,512]{1,0:T(8,128)(2,1)}, u32[]{:S(2)}) copy-start(bf16[128,512]{1,0:T(8,128)(2,1)} %param.26) | copy-start | bytes 393220
  7.2 64.5 %all-gather.6.cloned.1.call-start = ((), (), s32[]{:S(2)}) async-start(), calls=%async_computation.1 | async-start | bytes 2654208 | tf_op jit(solution)/shard_map/all_gather | solution.py:66
  15.9 2.4 copy-start.5
  15.9 2.4 copy-start.25
  15.9 2.4 copy-start.27
  17.0 120.7 %all-gather.8.cloned.1.call-start = ((), (), s32[]{:S(2)}) async-start(), calls=%async_computation.2 | async-start | bytes 2654208 | tf_op jit(solution)/shard_map/all_gather | solution.py:88
  75.2 3.1 copy-start.26
  78.1 2.6 copy-start.24
  81.1 7.4 %copy-start.14 = (bf16[12,96,128]{2,1,0:T(8,128)(2,1)}, bf16[12,96,128]{2,1,0:T(8,128)(2,1)S(1)}, u32[]{:S(2)}) copy-start(bf16[12,96,128]{2,1,0:T(8,128)(2,1)S(1)} %multiply_convert_fusion.4) | copy-start | bytes 884740
  83.0 5.5 %copy-start.22 = (bf16[128,128]{1,0:T(8,128)(2,1)S(1)}, bf16[128,128]{1,0:T(8,128)(2,1)}, u32[]{:S(2)}) copy-start(bf16[128,128]{1,0:T(8,128)(2,1)} %param.27) | copy-start | bytes 98308
  84.0 22.9 %copy-start.9 = (bf16[12,96,128]{2,1,0:T(8,128)(2,1)}, bf16[12,96,128]{2,1,0:T(8,128)(2,1)S(1)}, u32[]{:S(2)}) copy-start(bf16[12,96,128]{2,1,0:T(8,128)(2,1)S(1)} %get-tuple-element.22) | copy-start | bytes 884740
  84.9 22.0 %all-to-all-start = ((bf16[12,96,128]{2,0,1:T(8,128)(2,1)}), bf16[12,96,128]{2,0,1:T(8,128)(2,1)S(1)}, u32[]{:S(2)}, u32[]{:S(2)}) async-start(bf16[12,96,128]{2,0,1:T(8,128)(2,1)} %copy.49), calls=%async_computation | async-start | bytes 786432 | tf_op jit(solution)/shard_map/all_to_all | solution.py:83
  88.4 111.4 %all-gather.10.cloned.1.call-start = ((), (), s32[]{:S(2)}) async-start(), calls=%async_computation.3 | async-start | bytes 2654208 | tf_op jit(solution)/shard_map/all_gather | solution.py:106
  141.3 4.9 %copy-start.20 = (bf16[128,128]{1,0:T(8,128)(2,1)S(1)}, bf16[128,128]{1,0:T(8,128)(2,1)}, u32[]{:S(2)}) copy-start(bf16[128,128]{1,0:T(8,128)(2,1)} %param.29) | copy-start | bytes 98308
  141.3 4.9 %copy-start.23 = (f32[128]{0:T(128)S(1)}, f32[128]{0:T(128)}, u32[]{:S(2)}) copy-start(f32[128]{0:T(128)} %param.28) | copy-start | bytes 1540
  144.2 1.9 copy-start.4
  144.2 1.9 copy-start.7
  146.2 3.2 copy-start.11
  146.9 3.7 %copy-start.10 = (bf16[12,96,128]{2,1,0:T(8,128)(2,1)S(1)}, bf16[12,96,128]{2,1,0:T(8,128)(2,1)}, u32[]{:S(2)}) copy-start(bf16[12,96,128]{2,1,0:T(8,128)(2,1)} %copy-done.9) | copy-start | bytes 884740
  147.7 5.8 %copy-start.15 = (bf16[12,96,128]{2,1,0:T(8,128)(2,1)S(1)}, bf16[12,96,128]{2,1,0:T(8,128)(2,1)}, u32[]{:S(2)}) copy-start(bf16[12,96,128]{2,1,0:T(8,128)(2,1)} %copy-done.14) | copy-start | bytes 884740
  149.2 139.2 %all-reduce.7.cloned.1.call-start = ((), (), s32[]{:S(2)}) async-start(), calls=%async_computation.5 | async-start | bytes 133120 | tf_op jit(solution)/shard_map/psum | solution.py:119
  217.9 1.9 copy-start.16
  219.2 2.9 copy-start.8
  219.8 111.5 %all-gather.12.cloned.1.call-start = ((), (), s32[]{:S(2)}) async-start(), calls=%async_computation.4 | async-start | bytes 1179648 | tf_op jit(solution)/shard_map/all_gather | solution.py:118
  (10 other events, 11.3 us)
Sparse Core Ops, SparseCore 0:
  17.1 54.5 all-gather.5
  84.2 53.5 all-gather.7
  149.3 50.4 all-gather.9
  219.9 68.4 all-reduce.6
  291.0 40.2 all-gather.11
